TPU v7x, 512 devices: a whole 4x4x16 slice. The times are simulated.
512 devices in a mesh: row: 8 (over y, core), col: 16 (over z), depth: 4 (over x).
Axes of the slice: x: 4, y: 4, z: 16, core: 2. Of those that a mesh axis runs over, the one named last changes fastest.
Arguments:
- state_matrix: float32 [6144, 6144], P('row', 'col'), as said below
- gram_factor: float32 [6144, 256], P(('col', 'depth'), 'row'), as said below
Outputs:
- squared: float32 [6144, 6144], P('row', ('col', 'depth'))
- appended: float32 [6144, 256], P(('row', 'col', 'depth'))
- norm_ratio: float32 [256], replicated
Inputs may be any that keep to these rules, and one draw needn't show every extreme that they name: `gram_factor`: entries whose scale grows up to about ninefold along the rows; the columns differ in scale by up to tenfold. `state_matrix`: A real matrix with entries of order one on the diagonal and smaller ones elsewhere.
All inputs are finite; a program needn't handle non-finite values.
Results may differ from a plain program's by a relative error of at most 0.000073.
Values sent between devices are 32-bit elements; how exact they have to be, the bound alone decides.
A program may use at most 64 MiB of HBM per device.

v0:
```python
import functools

import jax
import jax.numpy as jnp
from jax import lax
from jax.sharding import Mesh
from jax.sharding import PartitionSpec as P

ROW = ("row_0", "row_1")
ROW_COL_DEPTH = ("row_0", "row_1", "col", "depth")


def sent_to_all(shard, axis):
    copies = jnp.broadcast_to(shard, (lax.axis_size(axis), *shard.shape))
    return lax.all_to_all(copies, axis, split_axis=0, concat_axis=0, tiled=True)


def laid_out(parts, dim):
    dims = list(parts.shape[1:])
    dims[dim] *= parts.shape[0]
    return jnp.moveaxis(parts, 0, dim).reshape(dims)


def gather_directly(shard, axis, dim):
    parts = sent_to_all(shard, axis)
    return laid_out(parts, dim)


def cut_along(shard, dim, devices):
    dims = shard.shape
    parts = shard.reshape(*dims[:dim], devices, dims[dim] // devices, *dims[dim + 1 :])
    return jnp.moveaxis(parts, dim, 0)


def sent_and_summed(shard, axis, dim):
    devices = lax.axis_size(axis)
    parts = lax.all_to_all(cut_along(shard, dim, devices), axis, 0, 0, tiled=True)
    return jnp.sum(parts, axis=0)


def by_axis(shard, axes):
    return functools.reduce(lax.psum, axes, shard)


def product(left, right):
    return jnp.dot(left, right, preferred_element_type=jnp.float32, precision=lax.Precision.HIGHEST)


def body(state_matrix, gram_factor):
    row_count = lax.axis_size(ROW)
    depth_count = lax.axis_size("depth")
    depth_index = lax.axis_index("depth")
    block_rows, block_cols = state_matrix.shape
    slab = block_cols // depth_count
    blocks_per_row = block_rows // block_cols
    own_columns = lax.dynamic_slice_in_dim(state_matrix, depth_index * slab, slab, 1)
    stacked = state_matrix.reshape(blocks_per_row, block_cols, block_cols)
    own_rows = lax.dynamic_slice_in_dim(stacked, depth_index * slab, slab, 1).reshape(
        blocks_per_row * slab, block_cols
    )
    column_block = gather_directly(own_rows, ROW, 0)
    factor_block = gather_directly(gram_factor, ROW, 1)
    partial_square = product(lax.all_gather(own_columns, "col", axis=1, tiled=True), column_block)
    factor_terms = product(own_columns, factor_block)
    new_rows = sent_and_summed(factor_terms, ("col", "depth"), 0)
    squared = sent_and_summed(partial_square, "depth", 1)
    new_sq = jnp.sum(new_rows * new_rows, axis=0)
    old_sq = jnp.sum(factor_block * factor_block, axis=0) * (1.0 / row_count)
    totals_new, totals_old = (by_axis(new_sq, ROW_COL_DEPTH), by_axis(old_sq, ROW_COL_DEPTH))
    norm_ratio = jnp.sqrt(totals_new) / jnp.sqrt(totals_old + 1e-06)
    return (squared, new_rows, norm_ratio)


def solution(mesh):
    split = Mesh(
        mesh.devices.reshape(4, 2, mesh.shape["col"], mesh.shape["depth"]),
        ("row_0", "row_1", "col", "depth"),
    )
    in_specs = (P(ROW, "col"), P(("col", "depth"), ROW))
    out_specs = (P(ROW, ("col", "depth")), P(ROW_COL_DEPTH, None), P())
    return jax.shard_map(body, mesh=split, in_specs=in_specs, out_specs=out_specs, check_vma=False)
```

profile of v0, /device:TPU:8, one launch (start us, length us, event | category | flops | bytes accessed | tf_op | source)
XLA Modules:
  0.0 209.6 jit_solution(1519927421017358025)
XLA Ops:
  7.2 0.0 copy-start
  7.2 0.0 all-gather.2.cloned.1.call-start
  7.2 1.2 copy-done
  8.4 0.2 constant_dynamic-slice_fusion.1
  8.6 0.9 copy.20
  9.5 0.0 all-gather.2.cloned.1.call-update
  9.5 1.4 broadcast_in_dim.7
  10.9 9.1 %all-to-all-start.2 = ((f32[8,96,32]{1,2,0:T(8,128)}), f32[8,96,32]{1,2,0:T(8,128)S(1)}, u32[]{:S(2)}, u32[]{:S(2)}) async-start(f32[8,96,32]{1,2,0:T(8,128)} %broadcast_in_dim.7), calls=%async_computation.2 | async-start | bytes 262144 | tf_op jit(solution)/shard_map/all_to_all | solution.py:15
  20.0 4.7 %all-to-all-done.2 = f32[8,96,32]{1,2,0:T(8,128)S(1)} async-done(((f32[8,96,32]{1,2,0:T(8,128)}), f32[8,96,32]{1,2,0:T(8,128)S(1)}, u32[]{:S(2)}, u32[]{:S(2)}) %all-to-all-start.2) | async-done | bytes 98336 | tf_op jit(solution)/shard_map/all_to_all | solution.py:15
  24.6 1.6 broadcast_in_dim.6
  26.3 0.0 copy-done.1
  26.3 5.0 %all-to-all-start = ((f32[8,192,384]{2,1,0:T(8,128)}), f32[8,192,384]{2,1,0:T(8,128)S(1)}, u32[]{:S(2)}, u32[]{:S(2)}) async-start(f32[8,192,384]{2,1,0:T(8,128)} %broadcast_in_dim.6), calls=%async_computation | async-start | bytes 4718592 | tf_op jit(solution)/shard_map/all_to_all | solution.py:15
  31.2 1.8 dot_general.15
  33.1 1.8 fusion.5
  34.9 1.4 copy.17
  36.3 23.5 %all-to-all-done = f32[8,192,384]{2,1,0:T(8,128)S(1)} async-done(((f32[8,192,384]{2,1,0:T(8,128)}), f32[8,192,384]{2,1,0:T(8,128)S(1)}, u32[]{:S(2)}, u32[]{:S(2)}) %all-to-all-start) | async-done | bytes 2359328 | tf_op jit(solution)/shard_map/all_to_all | solution.py:15
  59.8 14.6 %all-to-all-start.3 = ((f32[64,12,256]{2,1,0:T(8,128)}), f32[64,12,256]{2,1,0:T(8,128)}, u32[]{:S(2)}, u32[]{:S(2)}) async-start(f32[64,12,256]{2,1,0:T(8,128)} %copy.17), calls=%async_computation.3 | async-start | bytes 2097152 | tf_op jit(solution)/shard_map/all_to_all | solution.py:37
  74.4 2.0 copy.13
  76.4 57.4 %all-gather.2.cloned.1.call-done = f32[768,1536]{0,1:T(8,128)} async-done(((f32[768,96]{0,1:T(8,128)}), f32[768,1536]{0,1:T(8,128)}) %all-gather.2.cloned.1.call-update) | async-done | bytes 4718608 | tf_op jit(solution)/shard_map/all_gather | solution.py:63
  133.8 9.3 %fusion.2 = f32[4,768,96]{1,2,0:T(8,128)} fusion(f32[4,96,1536]{2,1,0:T(8,128)} %bitcast.25, f32[768,1536]{0,1:T(8,128)} %all-gather.2.cloned.1.call-done), kind=kOutput, calls=%fused_computation.2 | convolution fusion | flops 5435817984 | bytes 8257536 | tf_op jit(solution)/shard_map/dot_general | solution.py:46
  143.1 0.0 all-to-all-done.3
  143.1 4.1 %all-to-all-start.1 = ((f32[4,768,96]{1,2,0:T(8,128)}), f32[4,768,96]{1,2,0:T(8,128)S(1)}, u32[]{:S(2)}, u32[]{:S(2)}) async-start(f32[4,768,96]{1,2,0:T(8,128)} %fusion.2), calls=%async_computation.1 | async-start | bytes 2359296 | tf_op jit(solution)/shard_map/all_to_all | solution.py:37
  147.2 0.1 fusion.7
  147.3 0.1 mul.25
  147.4 1.3 reduce_sum.37
  148.7 9.2 %all-reduce.2 = (f32[256]{0:T(256)S(1)}, f32[256]{0:T(256)S(1)}) all-reduce(f32[256]{0:T(256)S(1)} %mul.25, f32[256]{0:T(256)S(1)} %multiply_reduce_fusion), channel_id=1, replica_groups=mesh['row_0'=4,'row_1'=2,'col'=16,'depth'=4] {'row_0'}, use_global_device_ids=true, to_apply=%region_8.0 | all-reduce | flops 512 | bytes 4096 | tf_op jit(solution)/shard_map/psum | solution.py:42
  157.9 2.5 %all-reduce.3 = (f32[256]{0:T(256)S(1)}, f32[256]{0:T(256)S(1)}) all-reduce(f32[256]{0:T(256)S(1)} %get-tuple-element.7, f32[256]{0:T(256)S(1)} %get-tuple-element.8), channel_id=1, replica_groups=mesh['row_0'=4,'row_1'=2,'col'=16,'depth'=4] {'row_1'}, use_global_device_ids=true, to_apply=%region_9.0 | all-reduce | flops 512 | bytes 4096 | tf_op jit(solution)/shard_map/psum | solution.py:42
  160.4 30.0 %all-reduce = (f32[256]{0:T(256)S(1)}, f32[256]{0:T(256)S(1)}) all-reduce(f32[256]{0:T(256)S(1)} %get-tuple-element.9, f32[256]{0:T(256)S(1)} %get-tuple-element.10), channel_id=1, replica_groups=mesh['row_0'=4,'row_1'=2,'col'=16,'depth'=4] {'col'}, use_global_device_ids=true, to_apply=%region_10.0 | all-reduce | flops 512 | bytes 4096 | tf_op jit(solution)/shard_map/psum | solution.py:42
  190.4 10.9 %all-reduce.1 = (f32[256]{0:T(256)S(1)}, f32[256]{0:T(256)S(1)}) all-reduce(f32[256]{0:T(256)S(1)} %get-tuple-element.3, f32[256]{0:T(256)S(1)} %get-tuple-element.4), channel_id=1, replica_groups=mesh['row_0'=4,'row_1'=2,'col'=16,'depth'=4] {'depth'}, use_global_device_ids=true, to_apply=%region_11.0 | all-reduce | flops 512 | bytes 4096 | tf_op jit(solution)/shard_map/psum | solution.py:42
  201.4 0.6 rsqrt_multiply_fusion
  201.9 0.0 all-to-all-done.1
  201.9 0.8 reduce_sum.36
  (10 shorter events, 0.1 us)
Async XLA Ops:
  7.2 1.3 copy-start
  7.2 126.6 %all-gather.2.cloned.1.call-start = ((), (), s32[]{:S(2)}) async-start(), calls=%async_computation.4 | async-start | bytes 5013504 | tf_op jit(solution)/shard_map/all_gather | solution.py:63
  8.6 17.6 %copy-start.1 = (f32[768,96]{1,0:T(8,128)}, f32[768,96]{1,0:T(8,128)S(1)}, u32[]{:S(2)}) copy-start(f32[768,96]{1,0:T(8,128)S(1)} %constant_dynamic-slice_fusion.1) | copy-start | bytes 884740
  10.9 13.8 %all-to-all-start.2 = ((f32[8,96,32]{1,2,0:T(8,128)}), f32[8,96,32]{1,2,0:T(8,128)S(1)}, u32[]{:S(2)}, u32[]{:S(2)}) async-start(f32[8,96,32]{1,2,0:T(8,128)} %broadcast_in_dim.7), calls=%async_computation.2 | async-start | bytes 262144 | tf_op jit(solution)/shard_map/all_to_all | solution.py:15
  24.6 1.6 copy-start.2
  26.3 33.5 %all-to-all-start = ((f32[8,192,384]{2,1,0:T(8,128)}), f32[8,192,384]{2,1,0:T(8,128)S(1)}, u32[]{:S(2)}, u32[]{:S(2)}) async-start(f32[8,192,384]{2,1,0:T(8,128)} %broadcast_in_dim.6), calls=%async_computation | async-start | bytes 4718592 | tf_op jit(solution)/shard_map/all_to_all | solution.py:15
  59.8 83.3 %all-to-all-start.3 = ((f32[64,12,256]{2,1,0:T(8,128)}), f32[64,12,256]{2,1,0:T(8,128)}, u32[]{:S(2)}, u32[]{:S(2)}) async-start(f32[64,12,256]{2,1,0:T(8,128)} %copy.17), calls=%async_computation.3 | async-start | bytes 2097152 | tf_op jit(solution)/shard_map/all_to_all | solution.py:37
  143.1 4.1 %copy-start.3 = (f32[8,96,32]{1,2,0:T(8,128)S(1)}, f32[8,96,32]{1,2,0:T(8,128)}, u32[]{:S(2)}) copy-start(f32[8,96,32]{1,2,0:T(8,128)} %copy-done.2) | copy-start | bytes 294916
  143.1 58.8 %all-to-all-start.1 = ((f32[4,768,96]{1,2,0:T(8,128)}), f32[4,768,96]{1,2,0:T(8,128)S(1)}, u32[]{:S(2)}, u32[]{:S(2)}) async-start(f32[4,768,96]{1,2,0:T(8,128)} %fusion.2), calls=%async_computation.1 | async-start | bytes 2359296 | tf_op jit(solution)/shard_map/all_to_all | solution.py:37
  148.7 54.0 %copy-start.4 = (f32[12,256]{1,0:T(8,128)}, f32[12,256]{1,0:T(8,128)S(1)}, u32[]{:S(2)}) copy-start(f32[12,256]{1,0:T(8,128)S(1)} %reduce_sum.37) | copy-start | bytes 36868
Sparse Core Ops, SparseCore 0:
  10.6 123.1 all-gather.1
where the time goes:
time: 210 us
  waiting for transfers between devices  85.5 us (41%)
  blocking collectives  52.6 us (25%)
  starting transfers between devices  32.8 us (16%)
  between operations  14.1 us (7%)
  matrix products  11.1 us (5%)
  local copies, waits for them, and re-layouts  10.6 us (5%)
  other arithmetic  2.82 us (1%)
    all_gather x1, waiting for transfers between devices, body(): lax.all_gather(own_columns, 'col', axis=1, tiled=True)  57.4 us
    psum x4, blocking collectives, by_axis(): return functools.reduce(lax.psum, axes, shard)  52.6 us
    all_to_all x2, waiting for transfers between devices, sent_to_all(): return lax.all_to_all(copies, axis, split_axis=0, concat_axis=0, tiled=True)  28.1 us
    all_to_all x2, starting transfers between devices, sent_and_summed(): lax.all_to_all(cut_along(shard, dim, devices), axis, 0, 0, tiled=True)  18.7 us
    all_to_all x2, starting transfers between devices, sent_to_all(): return lax.all_to_all(copies, axis, split_axis=0, concat_axis=0, tiled=True)  14 us
    dot_general x2, matrix products, product(): jnp.dot(left, right, preferred_element_type=jnp.float32, precision=lax.Pr...  11.1 us
    dot_general x3, local copies, waits for them, and re-layouts, product(): jnp.dot(left, right, preferred_element_type=jnp.float32, precision=lax.Pr...  5.23 us
  transfers between devices with their start and end apart: 5, of which 3 were waited for; matrix products, arithmetic and copies ran while one was open for 10% of the time, Pallas kernels for 0%

commit v1 on v0

v1 whole, which is shorter than its diff:
```python
import functools

import jax
import jax.numpy as jnp
from jax import lax
from jax.experimental import pallas as pl
from jax.experimental.pallas import tpu as pltpu
from jax.sharding import PartitionSpec as P

MESH = pl.DeviceIdType.MESH
NR, NC, ND = 8, 16, 4
SUBS = 4
F32 = jnp.float32
BF16 = jnp.bfloat16
NT = (((1,), (1,)), ((), ()))
NN = (((1,), (0,)), ((), ()))


def split(v):
    hi = v.astype(BF16)
    return hi, (v - hi.astype(F32)).astype(BF16)


def product3(a, b, dims):
    a_hi, a_lo = split(a)
    b_hi, b_lo = split(b)
    dot = functools.partial(lax.dot_general, dimension_numbers=dims, preferred_element_type=F32)
    return dot(a_hi, b_hi) + (dot(a_hi, b_lo) + dot(a_lo, b_hi))


def kernel(
    a_hbm, g_hbm, sq_hbm, app_hbm, norm_hbm,
    zg, blk, zin, zall, pst, r1, s1, ra, rb, rd, sb, app, sx, sr, sz, nrm, acc, stage, cout,
    lsem, zsend, zrecv, bsend, brecv, gsend, grecv_x, grecv_r, psend, precv1, precv2,
    ssend, srecv_x, srecv_r, srecv_z, csend, crecv, osem,
):
    r, z, d = lax.axis_index("row"), lax.axis_index("col"), lax.axis_index("depth")
    rows, width = blk.shape[1], blk.shape[2]
    part = rows // ND
    sub = part // SUBS
    partner = r + 1 - 2 * (r % 2)
    pos, grp = z % 4, z // 4
    up, down = (z + 1) % NC, (z + NC - 1) % NC

    def at(i, size):
        return pl.ds(pl.multiple_of(i * size, 8), size)

    def remote(src, dst, send, recv, **device):
        return pltpu.make_async_remote_copy(
            src_ref=src, dst_ref=dst, send_sem=send, recv_sem=recv, device_id=device, device_id_type=MESH
        )

    started = []

    def go(copy):
        copy.start()
        started.append(copy)

    load_block = pltpu.make_async_copy(a_hbm, blk.at[r], lsem.at[0])
    load_own = pltpu.make_async_copy(a_hbm.at[at(d, part), :], zg.at[z], lsem.at[1])
    load_gram = pltpu.make_async_copy(g_hbm, zin, lsem.at[2])
    load_own.start()
    load_gram.start()
    load_block.start()

    barrier = pltpu.get_barrier_semaphore()
    peers = [{"col": (z + k) % NC} for k in (1, 15, 2, 14, 3, 13)]
    peers += [{"depth": (d + k) % ND} for k in range(1, ND)]
    peers += [{"row": (r + k) % NR} for k in range(1, NR)]
    for peer in peers:
        pl.semaphore_signal(barrier, inc=1, device_id=peer, device_id_type=MESH)
    load_gram.wait()
    zall[r, d] = zin[...].T
    pl.semaphore_wait(barrier, len(peers))

    def hop(way, k, s):
        source = (z - k + NC) % NC if way == 0 else (z + k) % NC
        piece = zg.at[source, pl.ds(s * sub, sub), :]
        return remote(piece, piece, zsend.at[way, k, s], zrecv.at[way, k, s], col=up if way == 0 else down)

    def travels(way, k, s):
        return k < 7 or (s < SUBS // 2) == (way == 0)

    def ring(k, subs=range(SUBS)):
        for s in subs:
            for way in (0, 1):
                if k > 0 and travels(way, k - 1, s):
                    hop(way, k - 1, s).wait_recv()
                if k < 8 and travels(way, k, s):
                    go(hop(way, k, s))

    n_sent = [0]

    def block_piece(b, q):
        return blk.at[b, at(q, part), :]

    def block_send(b, q, **device):
        go(remote(block_piece(b, q), block_piece(b, q), bsend.at[n_sent[0]], brecv.at[b, q], **device))
        n_sent[0] += 1

    def block_wait(b, q):
        remote(block_piece(b, q), block_piece(b, q), bsend.at[0], brecv.at[b, q], row=partner).wait_recv()

    q0, q1, q2, q3 = d, (d + 1) % ND, (d + 2) % ND, (d + 3) % ND
    above, below, across = (r + 2) % NR, (r + NR - 2) % NR, (r + 4) % NR
    right, left = (d + 1) % ND, (d + ND - 1) % ND

    def block_event_1():
        block_wait(below, q0)
        block_send(below, q0, row=above)
        block_send(below, q0, depth=right)
        block_send(below, q0, row=partner)
        block_wait(above, q1)
        block_send(above, q1, row=below)
        block_send(above, q1, depth=left)
        block_send(above, q1, row=partner)

    def block_event_2():
        block_wait(below, q1)
        block_send(below, q1, depth=left)
        block_send(below, q1, row=partner)
        block_wait(above, q0)
        block_send(above, q0, depth=right)
        block_send(above, q0, row=partner)
        block_wait(below, q3)
        block_send(below, q3, row=partner)
        block_wait(above, q2)
        block_send(above, q2, row=partner)

    def block_event_3():
        block_wait(across, q0)
        block_send(across, q0, depth=right)
        block_send(across, q0, row=partner)
        block_wait(across, q1)
        block_send(across, q1, depth=left)
        block_send(across, q1, row=partner)
        block_wait(above, q3)
        block_send(above, q3, row=partner)
        block_wait(below, q2)
        block_send(below, q2, row=partner)

    def block_event_4():
        block_wait(across, q3)
        block_send(across, q3, row=partner)
        block_wait(across, q2)
        block_send(across, q2, row=partner)
        for b in (partner, (partner + 2) % NR, (partner + 4) % NR, (partner + 6) % NR):
            for q in range(ND):
                block_wait(b, q)

    def chunk(source):
        left_op = zg[source]
        right_op = blk[source // 2, at(source % 2, width), :]
        acc[...] += product3(left_op, right_op, NN)

    def chunks(k):
        def one(i, _):
            chunk((z + NC + k - 2 * k * i) % NC)
            return 0

        lax.fori_loop(0, 2, one, 0)

    load_own.wait()
    ring(0)
    for k in range(1, ND):
        peer = (d + k) % ND
        go(remote(zall.at[r, d], zall.at[r, d], gsend.at[k], grecv_x.at[d], depth=peer))
    load_block.wait()
    block_send(r, q0, row=above)
    block_send(r, q1, row=below)
    block_send(r, q1, row=above)
    block_send(r, q0, row=below)
    for q in range(ND):
        block_send(r, q, row=partner)

    for k in range(1, ND):
        peer = (d + k) % ND
        remote(zall.at[r, peer], zall.at[r, peer], gsend.at[0], grecv_x.at[peer], depth=peer).wait_recv()
    for k in range(1, NR):
        peer = (r + k) % NR
        go(remote(zall.at[r], zall.at[r], gsend.at[3 + k], grecv_r.at[r], row=peer))
    for k in range(1, NR):
        peer = (r + k) % NR
        remote(zall.at[peer], zall.at[peer], gsend.at[0], grecv_r.at[peer], row=peer).wait_recv()
    rank = NR * zin.shape[1]
    factor = jnp.concatenate([zall[:, x].reshape(rank, zin.shape[0]) for x in range(ND)], axis=1)
    own_rows = app.shape[0]
    for b in range(ND):
        partial = product3(blk[r, pl.ds(b * part, part), :], factor, NT)
        for i in range(part // own_rows):
            pst[i % ND, i // ND, b] = partial[i * own_rows : (i + 1) * own_rows]
    squares = factor * factor
    s_hi, s_lo = split(squares)
    ones = jnp.ones((8, width), BF16)
    old = lax.dot_general(ones, s_hi, NT, preferred_element_type=F32) + lax.dot_general(
        ones, s_lo, NT, preferred_element_type=F32
    )
    sx[d, 2] = old[0, :128]
    sx[d, 3] = old[0, 128:]
    for k in range(1, 4):
        q = (pos + k) % 4
        go(remote(pst.at[d, q], r1.at[pos], psend.at[k], precv1.at[pos], col=grp * 4 + q))

    ring(1)
    block_event_1()
    ring(2)
    block_event_2()
    total = pst[d, pos]
    for k in range(1, 4):
        q = (pos + k) % 4
        remote(r1.at[q], r1.at[q], psend.at[0], precv1.at[q], col=up).wait_recv()
        total = total + r1[q]
    s1[...] = total
    far_up, far_down = (z + 4) % NC, (z + NC - 4) % NC
    go(remote(s1.at[(grp + 2) % 4], ra, psend.at[4], precv2.at[0], col=far_down))
    go(remote(s1.at[(grp + 1) % 4], rd, psend.at[5], precv2.at[1], col=far_up))
    ring(3)
    block_event_3()
    remote(ra, ra, psend.at[0], precv2.at[0], col=up).wait_recv()
    sb[...] = ra[...] + s1[(grp + 3) % 4]
    go(remote(sb, rb, psend.at[6], precv2.at[2], col=far_down))
    acc[...] = jnp.zeros_like(acc)
    ring(4)
    block_event_4()
    chunk(z)
    chunks(1)
    remote(rd, rd, psend.at[0], precv2.at[1], col=up).wait_recv()
    remote(rb, rb, psend.at[0], precv2.at[2], col=up).wait_recv()
    new = s1[grp] + rd[...] + rb[...]
    app[...] = new
    new_sq = jnp.sum(new * new, axis=0, keepdims=True)
    sx[d, 0] = new_sq[0, :128]
    sx[d, 1] = new_sq[0, 128:]
    store_app = pltpu.make_async_copy(app, app_hbm, osem.at[0])
    store_app.start()
    for k in range(1, ND):
        go(remote(sx.at[d], sx.at[d], ssend.at[k], srecv_x.at[d], depth=(d + k) % ND))
    ring(5, range(2))
    chunks(2)
    ring(5, range(2, SUBS))
    chunks(3)
    for k in range(1, ND):
        q = (d + k) % ND
        remote(sx.at[q], sx.at[q], ssend.at[0], srecv_x.at[q], depth=q).wait_recv()
    sr[r] = jnp.sum(sx[...], axis=0)
    for k in range(1, NR):
        go(remote(sr.at[r], sr.at[r], ssend.at[3 + k], srecv_r.at[r], row=(r + k) % NR))
    ring(6, range(2))
    chunks(4)
    for k in range(1, NR):
        q = (r + k) % NR
        remote(sr.at[q], sr.at[q], ssend.at[0], srecv_r.at[q], row=q).wait_recv()
    sz[z] = jnp.sum(sr[...], axis=0)
    for k in range(1, NC):
        go(remote(sz.at[z], sz.at[z], ssend.at[10 + k], srecv_z.at[z], col=(z + k) % NC))
    ring(6, range(2, SUBS))
    chunks(5)
    ring(7, range(2))
    chunks(6)
    ring(7, range(2, SUBS))
    chunks(7)
    ring(8)
    chunk((z + 8) % NC)

    wide = cout.shape[2]
    for x in range(ND):
        stage[x] = acc[:, x * wide : (x + 1) * wide]
    for k in range(1, ND):
        q = (d + k) % ND
        go(remote(stage.at[q], cout.at[d], csend.at[k], crecv.at[d], depth=q))
    store_own = pltpu.make_async_copy(stage.at[d], sq_hbm.at[at(d, part), :], osem.at[1])
    store_own.start()

    for k in range(1, NC):
        q = (z + k) % NC
        remote(sz.at[q], sz.at[q], ssend.at[0], srecv_z.at[q], col=q).wait_recv()
    sums = jnp.sum(sz[...], axis=0)
    nrm[...] = jnp.sqrt(sums[0:2]) / jnp.sqrt(sums[2:4] * (1.0 / (NR * ND)) + 1e-06)
    store_norm = pltpu.make_async_copy(nrm, norm_hbm, osem.at[2])
    store_norm.start()
    stores = [store_app, store_own, store_norm]
    for k in range(1, ND):
        q = (d + k) % ND
        remote(cout.at[q], cout.at[q], csend.at[0], crecv.at[q], depth=q).wait_recv()
        store = pltpu.make_async_copy(cout.at[q], sq_hbm.at[at(q, part), :], osem.at[2 + k])
        store.start()
        stores.append(store)
    for copy in started:
        copy.wait_send()
    for store in stores:
        store.wait()


def body(state_matrix, gram_factor):
    rows, width = state_matrix.shape
    factor_rows, factor_cols = gram_factor.shape
    part = rows // ND
    rank = factor_cols * NR
    wide = width // ND
    own_rows = rows // (NC * ND)
    dma = pltpu.SemaphoreType.DMA
    vmem = lambda *shape: pltpu.VMEM(shape, F32)
    squared, appended, norm = pl.pallas_call(
        kernel,
        out_shape=(
            jax.ShapeDtypeStruct((rows, wide), F32),
            jax.ShapeDtypeStruct((own_rows, rank), F32),
            jax.ShapeDtypeStruct((2, rank // 2), F32),
        ),
        in_specs=[pl.BlockSpec(memory_space=pl.ANY)] * 2,
        out_specs=[pl.BlockSpec(memory_space=pl.ANY)] * 3,
        scratch_shapes=[
            vmem(NC, part, width),
            vmem(NR, rows, width),
            vmem(factor_rows, factor_cols),
            vmem(NR, ND, factor_cols, factor_rows),
            vmem(ND, 4, 4, own_rows, rank),
            vmem(4, 4, own_rows, rank),
            vmem(4, own_rows, rank),
            vmem(own_rows, rank),
            vmem(own_rows, rank),
            vmem(own_rows, rank),
            vmem(own_rows, rank),
            vmem(own_rows, rank),
            vmem(ND, 4, 128),
            vmem(NR, 4, 128),
            vmem(NC, 4, 128),
            vmem(2, 128),
            vmem(part, width),
            vmem(ND, part, wide),
            vmem(ND, part, wide),
            dma((3,)),
            dma((2, 8, SUBS)),
            dma((2, 8, SUBS)),
            dma((40,)),
            dma((NR, ND)),
            dma((12,)),
            dma((ND,)),
            dma((NR,)),
            dma((8,)),
            dma((4,)),
            dma((3,)),
            dma((26,)),
            dma((ND,)),
            dma((NR,)),
            dma((NC,)),
            dma((ND,)),
            dma((ND,)),
            dma((6,)),
        ],
        compiler_params=pltpu.CompilerParams(
            collective_id=0, has_side_effects=True, vmem_limit_bytes=60 * 1024 * 1024
        ),
    )(state_matrix, gram_factor)
    return squared, appended, norm.reshape(rank)


def solution(mesh):
    in_specs = (P("row", "col"), P(("col", "depth"), "row"))
    out_specs = (P("row", ("col", "depth")), P(("row", "col", "depth"), None), P())
    return jax.shard_map(body, mesh=mesh, in_specs=in_specs, out_specs=out_specs, check_vma=False)
```

time: 210 us -> 103 us (0.49)
  the two profiles are of different devices: /device:TPU:8 before, /device:TPU:1 now
where the time goes in v1:
time: 103 us
  Pallas kernels  96.5 us (94%)
  local copies, waits for them, and re-layouts  5.86 us (6%)
    pallas_call x1, Pallas kernels, body(): pl.pallas_call(kernel, out_shape=(jax.ShapeDtypeStruct((rows, wide), F32)...  96.5 us
    unnamed x4, local copies, waits for them, and re-layouts  5.86 us

profile of v1, /device:TPU:1, one launch (start us, length us, event | category | flops | bytes accessed | tf_op | source)
XLA Modules:
  0.0 103.0 jit_solution(3859042706927874919)
XLA Ops:
  0.6 1.4 %copy.5.g_hbm = f32[96,32]{1,0:T(8,128)} copy(f32[96,32]{0,1:T(8,128)} %param.3) | data formatting | bytes 24576 | tf_op args[1]
  2.1 96.5 %shard_map.49 = (f32[768,96]{1,0:T(8,128)}, f32[12,256]{1,0:T(8,128)}, f32[2,128]{1,0:T(2,128)}) custom-call(f32[768,384]{1,0:T(8,128)} %a_hbm.1, f32[96,32]{1,0:T(8,128)} %copy.5.g_hbm), custom_call_target="tpu_custom_call" | custom-call | tf_op jit(solution)/shard_map/pallas_call | solution.py:303
  98.6 1.9 %copy.6 = f32[768,96]{0,1:T(8,128)} copy(f32[768,96]{1,0:T(8,128)} %get-tuple-element.9) | data formatting | bytes 589824
  100.5 1.3 %copy.9 = f32[12,256]{1,0:T(8,128)} copy(f32[12,256]{1,0:T(8,128)} %get-tuple-element.16) | data formatting | bytes 24576
  101.8 1.2 %copy.10 = f32[256]{0:T(256)} copy(f32[256]{0:T(256)} %bitcast.1) | data formatting | bytes 2048

commit v2 on v1

v2 whole, which is shorter than its diff:
```python
import functools

import jax
import jax.numpy as jnp
from jax import lax
from jax.experimental import pallas as pl
from jax.experimental.pallas import tpu as pltpu
from jax.sharding import PartitionSpec as P

MESH = pl.DeviceIdType.MESH
NR, NC, ND = 8, 16, 4
SUBS = 6
EARLY = range(4)
LATE = range(4, 6)
LANES = 128
F32 = jnp.float32
BF16 = jnp.bfloat16
NT = (((1,), (1,)), ((), ()))
NN = (((1,), (0,)), ((), ()))


def split(v):
    hi = v.astype(BF16)
    return hi, (v - hi.astype(F32)).astype(BF16)


def product3(a, b, dims):
    a_hi, a_lo = split(a)
    b_hi, b_lo = split(b)
    dot = functools.partial(lax.dot_general, dimension_numbers=dims, preferred_element_type=F32)
    return dot(a_hi, b_hi) + (dot(a_hi, b_lo) + dot(a_lo, b_hi))


def kernel(
    a_hbm, g_hbm, cout_e, cout_l, app, nrm,
    zg, blk, zall, pst, r1, s1, r2, sx, sr, plane, sz, both, acc, stage_e, stage_l,
    lsem, zsend, zrecv, bsend, brecv, gsend, grecv_x, grecv_r, psend, precv1, precv2,
    ssend, srecv_x, srecv_r, srecv_z, srecv_c, csend, crecv_e, crecv_l, token,
):
    r, z, d = lax.axis_index("row"), lax.axis_index("col"), lax.axis_index("depth")
    rows, width = blk.shape[1], blk.shape[2]
    part = rows // ND
    sub = part // SUBS
    first = sub * len(EARLY)
    core = r % 2
    partner = r + 1 - 2 * core
    pos, grp = z % 4, z // 4
    up, down = (z + 1) % NC, (z + NC - 1) % NC
    above, below, across = (r + 2) % NR, (r + NR - 2) % NR, (r + 4) % NR
    right, left = (d + 1) % ND, (d + ND - 1) % ND

    def at(i, size):
        return pl.ds(pl.multiple_of(i * size, 8), size)

    def remote(src, dst, send, recv, **device):
        return pltpu.make_async_remote_copy(
            src_ref=src, dst_ref=dst, send_sem=send, recv_sem=recv, device_id=device, device_id_type=MESH
        )

    started = []

    def go(copy):
        copy.start()
        started.append(copy)

    def arrived(ref, recv):
        remote(ref, ref, csend.at[0], recv, row=partner).wait_recv()

    load_own = pltpu.make_async_copy(a_hbm.at[at(d, part), :], zg.at[z], lsem.at[0])
    load_gram = pltpu.make_async_copy(g_hbm, zall.at[r, d], lsem.at[1])
    load_block = pltpu.make_async_copy(a_hbm, blk.at[r], lsem.at[2])
    load_own.start()
    load_gram.start()
    load_block.start()

    barrier = pltpu.get_barrier_semaphore()
    peers = [{"col": (z + k) % NC} for k in (1, 15, 2, 14, 3, 13)]
    peers += [{"depth": (d + k) % ND} for k in range(1, ND)]
    peers += [{"row": (r + k) % NR} for k in range(1, NR)]
    for peer in peers:
        pl.semaphore_signal(barrier, inc=1, device_id=peer, device_id_type=MESH)
    acc[...] = jnp.zeros_like(acc)
    load_own.wait()
    load_gram.wait()
    load_block.wait()
    pl.semaphore_wait(barrier, len(peers))

    def piece(way, k, s):
        source = (z - k + NC) % NC if way == 0 else (z + k) % NC
        return zg.at[source, pl.ds(s * sub, sub), :]

    def travels(way, k, s):
        return k < 7 or s % 2 == way

    def ring(k, subs):
        for s in subs:
            for way in (0, 1):
                if k > 0 and travels(way, k - 1, s):
                    arrived(piece(way, k, s), zrecv.at[way, k - 1, s])
                if k < 8 and travels(way, k, s):
                    ref = piece(way, k, s)
                    go(remote(ref, ref, zsend.at[way, k, s], zrecv.at[way, k, s], col=up if way == 0 else down))

    n_sent = [0]

    def block_piece(b, q):
        return blk.at[b, at(q, part), :]

    def block_send(b, q, **device):
        go(remote(block_piece(b, q), block_piece(b, q), bsend.at[n_sent[0]], brecv.at[b, q], **device))
        n_sent[0] += 1

    def block_wait(b, q):
        arrived(block_piece(b, q), brecv.at[b, q])

    q0, q1, q2, q3 = d, (d + 1) % ND, (d + 2) % ND, (d + 3) % ND

    def block_event_1():
        block_wait(below, q0)
        block_send(below, q0, row=above)
        block_send(below, q0, depth=right)
        block_send(below, q0, row=partner)
        block_wait(above, q1)
        block_send(above, q1, row=below)
        block_send(above, q1, depth=left)
        block_send(above, q1, row=partner)

    def block_event_2():
        block_wait(below, q1)
        block_send(below, q1, depth=left)
        block_send(below, q1, row=partner)
        block_wait(above, q0)
        block_send(above, q0, depth=right)
        block_send(above, q0, row=partner)
        block_wait(below, q3)
        block_send(below, q3, row=partner)
        block_wait(above, q2)
        block_send(above, q2, row=partner)

    def block_event_3():
        block_wait(across, q0)
        block_send(across, q0, depth=right)
        block_send(across, q0, row=partner)
        block_wait(across, q1)
        block_send(across, q1, depth=left)
        block_send(across, q1, row=partner)
        block_wait(above, q3)
        block_send(above, q3, row=partner)
        block_wait(below, q2)
        block_send(below, q2, row=partner)

    def block_event_4():
        block_wait(across, q3)
        block_send(across, q3, row=partner)
        block_wait(across, q2)
        block_send(across, q2, row=partner)
        for b in (partner, (partner + 2) % NR, (partner + 4) % NR, (partner + 6) % NR):
            for q in range(ND):
                block_wait(b, q)

    def chunk(source, lo, hi):
        left_op = zg[source, lo:hi]
        right_op = blk[source // 2, at(source % 2, width), :]
        acc[lo:hi] += product3(left_op, right_op, NN)

    def chunks(k, lo=0, hi=part):
        def one(i, _):
            chunk((z + NC + k - 2 * k * i) % NC, lo, hi)
            return 0

        lax.fori_loop(0, 2, one, 0)

    ring(0, EARLY)
    for k in range(1, ND):
        go(remote(zall.at[r, d], zall.at[r, d], gsend.at[k], grecv_x.at[d], depth=(d + k) % ND))
    ring(0, LATE)
    for k in range(1, ND):
        q = (d + k) % ND
        arrived(zall.at[r, q], grecv_x.at[q])
    for k, peer in enumerate((above, below, across, partner)):
        go(remote(zall.at[r], zall.at[r], gsend.at[4 + k], grecv_r.at[r], row=peer))
    block_send(r, q0, row=above)
    block_send(r, q1, row=below)
    block_send(r, q1, row=above)
    block_send(r, q0, row=below)
    for q in range(ND):
        block_send(r, q, row=partner)

    ring(1, EARLY)
    ring(1, LATE)
    for k, peer in enumerate((above, below, across)):
        arrived(zall.at[peer], grecv_r.at[peer])
        go(remote(zall.at[peer], zall.at[peer], gsend.at[8 + k], grecv_r.at[peer], row=partner))
    ring(2, EARLY)
    far = [(z + 5) % NC, (z + NC - 5) % NC]
    for peer in far:
        pl.semaphore_signal(token, inc=1, device_id={"col": peer}, device_id_type=MESH)

    for peer in (partner, (partner + 2) % NR, (partner + 4) % NR, (partner + 6) % NR):
        arrived(zall.at[peer], grecv_r.at[peer])
    rank = NR * zall.shape[2]
    factor = jnp.concatenate([zall[:, x].reshape(rank, zall.shape[3]) for x in range(ND)], axis=1)
    own = app.shape[0]
    for b in range(ND):
        partial = product3(blk[r, pl.ds(b * part, part), :], factor, NT)
        for i in range(part // own):
            value = partial[i * own : (i + 1) * own]
            pst[i % ND, i // ND, b, 0:own] = value[:, :LANES]
            pst[i % ND, i // ND, b, own : 2 * own] = value[:, LANES:]
    s_hi, s_lo = split(factor * factor)
    ones = jnp.ones((8, width), BF16)
    old = lax.dot_general(ones, s_hi, NT, preferred_element_type=F32) + lax.dot_general(
        ones, s_lo, NT, preferred_element_type=F32
    )
    sx[d, 2] = old[0, :LANES]
    sx[d, 3] = old[0, LANES:]
    for k in range(1, 4):
        q = (pos + k) % 4
        go(remote(pst.at[d, q], r1.at[pos], psend.at[k - 1], precv1.at[pos], col=grp * 4 + q))

    ring(2, LATE)
    block_event_1()
    ring(3, EARLY)
    ring(3, LATE)
    block_event_2()
    total = pst[d, pos]
    for k in range(1, 4):
        q = (pos + k) % 4
        arrived(r1.at[q], precv1.at[q])
        total = total + r1[q]
    s1[...] = total
    pl.semaphore_wait(token, 2)
    for k in range(1, 4):
        q = (grp + k) % 4
        go(remote(s1.at[q], r2.at[grp], psend.at[2 + k], precv2.at[grp], col=q * 4 + pos))
    ring(4, EARLY)
    ring(5, EARLY)
    ring(4, LATE)
    block_event_3()
    ring(6, EARLY)
    new = s1[grp]
    for k in range(1, 4):
        q = (grp + k) % 4
        arrived(r2.at[q], precv2.at[q])
        new = new + r2[q]
    app[:, :LANES] = new[:own]
    app[:, LANES:] = new[own:]
    squares = new * new
    sx[d, 0] = jnp.sum(squares[:own], axis=0)
    sx[d, 1] = jnp.sum(squares[own:], axis=0)
    for k in range(1, ND):
        go(remote(sx.at[d], sx.at[d], ssend.at[k], srecv_x.at[d], depth=(d + k) % ND))
    block_event_4()
    chunk(z, 0, part)
    chunks(1)
    ring(5, LATE)
    for k in range(1, ND):
        q = (d + k) % ND
        arrived(sx.at[q], srecv_x.at[q])
    sr[r] = jnp.sum(sx[...], axis=0)
    for k in range(1, NR):
        go(remote(sr.at[r], sr.at[r], ssend.at[3 + k], srecv_r.at[r], row=(r + k) % NR))
    chunks(2)
    chunks(3)
    ring(7, EARLY)
    for k in range(1, NR):
        q = (r + k) % NR
        arrived(sr.at[q], srecv_r.at[q])
    sums = jnp.sum(sr[...], axis=0)
    plane[0] = sums[0:2]
    plane[1] = sums[2:4]
    sz[z] = plane[core]
    for k in range(1, NC):
        go(remote(sz.at[z], sz.at[z], ssend.at[10 + k], srecv_z.at[z], col=(z + k) % NC))
    chunks(4)
    chunks(5)
    ring(6, LATE)
    chunks(6)
    chunks(7, 0, first)
    ring(8, EARLY)
    chunk((z + 8) % NC, 0, first)

    wide = width // ND
    turned = acc[0:first].T
    for x in range(ND):
        stage_e[x] = turned[x * wide : (x + 1) * wide]
    for k in (2, 1, 3):
        q = (d + k) % ND
        go(remote(stage_e.at[q], cout_e.at[d], csend.at[k], crecv_e.at[d], depth=q))
    cout_e[d] = stage_e[d]
    ring(7, LATE)
    chunks(7, first, part)
    ring(8, LATE)
    chunk((z + 8) % NC, first, part)
    turned = acc[first:part].T
    for x in range(ND):
        block = turned[x * wide : (x + 1) * wide]
        stage_l[x] = jnp.concatenate([block[: wide // 2], block[wide // 2 :]], axis=1)
    for k in (2, 1, 3):
        q = (d + k) % ND
        go(remote(stage_l.at[q], cout_l.at[d], csend.at[3 + k], crecv_l.at[d], depth=q))
    cout_l[d] = stage_l[d]

    for k in range(1, NC):
        q = (z + k) % NC
        arrived(sz.at[q], srecv_z.at[q])
    both[core] = jnp.sum(sz[...], axis=0)
    go(remote(both.at[core], both.at[core], ssend.at[26], srecv_c, row=partner))
    for copy in started:
        copy.wait_send()
    arrived(both.at[1 - core], srecv_c)
    nrm[...] = jnp.sqrt(both[0]) / jnp.sqrt(both[1] * (1.0 / (NR * ND)) + 1e-06)
    for k in range(1, ND):
        q = (d + k) % ND
        arrived(cout_e.at[q], crecv_e.at[q])
        arrived(cout_l.at[q], crecv_l.at[q])


def finish(early, late, app_in, nrm_in, sq, app, nrm):
    half = early.shape[1] // 2
    app[...] = app_in[...]
    nrm[...] = nrm_in[...]
    for i in range(0, ND, 2):
        e0, e1 = early[i], early[i + 1]
        l0, l1 = late[i], late[i + 1]
        base = i * 3 * LANES // 2
        sq[:, base : base + LANES] = e0
        l0_cols = jnp.concatenate([l0[:, :64], l0[:, 64:]], axis=0)
        l1_cols = jnp.concatenate([l1[:, :64], l1[:, 64:]], axis=0)
        sq[:, base + LANES : base + 2 * LANES] = jnp.concatenate([l0_cols, e1[:, :64]], axis=1)
        sq[:, base + 2 * LANES : base + 3 * LANES] = jnp.concatenate([e1[:, 64:], l1_cols], axis=1)


def body(state_matrix, gram_factor):
    rows, width = state_matrix.shape
    factor_rows, factor_cols = gram_factor.shape
    part = rows // ND
    rank = factor_cols * NR
    wide = width // ND
    own = rows // (NC * ND)
    dma = pltpu.SemaphoreType.DMA
    vmem = lambda *shape: pltpu.VMEM(shape, F32)
    shape = lambda *dims: jax.ShapeDtypeStruct(dims, F32)
    whole = pl.BlockSpec(memory_space=pltpu.VMEM)
    parts = pl.pallas_call(
        kernel,
        out_shape=(shape(ND, wide, LANES), shape(ND, wide // 2, LANES), shape(own, rank), shape(2, LANES)),
        in_specs=[pl.BlockSpec(memory_space=pltpu.HBM)] * 2,
        out_specs=[whole] * 4,
        scratch_shapes=[
            vmem(NC, part, width),
            vmem(NR, rows, width),
            vmem(NR, ND, factor_cols, factor_rows),
            vmem(ND, 4, 4, 2 * own, LANES),
            vmem(4, 4, 2 * own, LANES),
            vmem(4, 2 * own, LANES),
            vmem(4, 2 * own, LANES),
            vmem(ND, 4, LANES),
            vmem(NR, 4, LANES),
            vmem(2, 2, LANES),
            vmem(NC, 2, LANES),
            vmem(2, 2, LANES),
            vmem(part, width),
            vmem(ND, wide, LANES),
            vmem(ND, wide // 2, LANES),
            dma((3,)),
            dma((2, 8, SUBS)),
            dma((2, 8, SUBS)),
            dma((40,)),
            dma((NR, ND)),
            dma((12,)),
            dma((ND,)),
            dma((NR,)),
            dma((8,)),
            dma((4,)),
            dma((4,)),
            dma((28,)),
            dma((ND,)),
            dma((NR,)),
            dma((NC,)),
            dma,
            dma((8,)),
            dma((ND,)),
            dma((ND,)),
            pltpu.SemaphoreType.REGULAR,
        ],
        compiler_params=pltpu.CompilerParams(
            collective_id=0, has_side_effects=True, vmem_limit_bytes=55900000
        ),
    )(state_matrix, gram_factor.T)
    squared, appended, norm = pl.pallas_call(
        finish,
        out_shape=(shape(wide, rows), shape(own, rank), shape(2, LANES)),
        in_specs=[whole] * 4,
        out_specs=[whole] * 3,
        compiler_params=pltpu.CompilerParams(vmem_limit_bytes=8 * 1024 * 1024),
    )(*parts)
    return squared.T, appended, norm.reshape(rank)


def solution(mesh):
    in_specs = (P("row", "col"), P(("col", "depth"), "row"))
    out_specs = (P("row", ("col", "depth")), P(("row", "col", "depth"), None), P())
    return jax.shard_map(body, mesh=mesh, in_specs=in_specs, out_specs=out_specs, check_vma=False)
```

time: 103 us -> 83.6 us (0.81)
  Pallas kernels: 96.5 us -> 81.7 us
  local copies, waits for them, and re-layouts: 5.86 us -> 0.71 us
    pallas_call x1 -> x2, Pallas kernels: 96.5 us -> 81.7 us  [the longest x1 80.9 us: body(): pl.pallas_call(kernel, out_shape=(shape(ND, wide, LANES), shape(ND, wide...]
    unnamed x4 -> x2, local copies, waits for them, and re-layouts: 5.86 us -> 0.71 us
where the time goes in v2:
time: 83.6 us; the launch traced here: 83.1 us
  Pallas kernels  81.7 us (98%)
    pallas_call x1, Pallas kernels, body(): pl.pallas_call(kernel, out_shape=(shape(ND, wide, LANES), shape(ND, wide...  80.9 us

profile of v2, /device:TPU:1, one launch (start us, length us, event | category | flops | bytes accessed | tf_op | source)
XLA Modules:
  0.0 83.1 jit_solution(3560485303084111698)
XLA Ops:
  0.6 0.0 copy-start
  0.6 0.7 copy-done
  1.3 80.9 %shard_map.49 = (f32[4,96,128]{2,1,0:T(8,128)S(1)}, f32[4,48,128]{2,1,0:T(8,128)S(1)}, f32[12,256]{1,0:T(8,128)S(1)}, f32[2,128]{1,0:T(2,128)S(1)}) custom-call(f32[768,384]{1,0:T(8,128)} %a_hbm.1, f32[32,96]{1,0:T(8,128)S(1)} %bitcast.3), custom_call_target="tpu_custom_call" | custom-call | tf_op jit(solution)/shard_map/pallas_call | solution.py:345
  82.2 0.9 %shard_map.50 = (f32[96,768]{1,0:T(8,128)}, f32[12,256]{1,0:T(8,128)}, f32[2,128]{1,0:T(2,128)}) custom-call(f32[4,96,128]{2,1,0:T(8,128)S(1)} %get-tuple-element.10.early, f32[4,48,128]{2,1,0:T(8,128)S(1)} %get-tuple-element.11.late, f32[12,256]{1,0:T(8,128)S(1)} %get-tuple-element.12.app_in, f32[2,128]{1,0:T(2,128)S(1)} %get-tuple-element.13.nrm_in), custom_call_target="tpu_custom_call" | custom-call | tf_op jit(solution)/shard_map/pallas_call | solution.py:391
Async XLA Ops:
  0.6 0.7 copy-start

commit v3 on v2

--- a/solution.py
+++ b/solution.py
@@ -33,9 +33,9 @@
 
 def kernel(
     a_hbm, g_hbm, cout_e, cout_l, app, nrm,
-    zg, blk, zall, pst, r1, s1, r2, sx, sr, plane, sz, both, acc, stage_e, stage_l,
+    zg, blk, zall, pst, r1, s1, r2, sx, plane, sz, both, acc, stage_e, stage_l,
     lsem, zsend, zrecv, bsend, brecv, gsend, grecv_x, grecv_r, psend, precv1, precv2,
-    ssend, srecv_x, srecv_r, srecv_z, srecv_c, csend, crecv_e, crecv_l, token,
+    ssend, srecv_x, srecv_z, srecv_c, csend, crecv_e, crecv_l, token_2, token_4,
 ):
     r, z, d = lax.axis_index("row"), lax.axis_index("col"), lax.axis_index("depth")
     rows, width = blk.shape[1], blk.shape[2]
@@ -45,6 +45,7 @@
     core = r % 2
     partner = r + 1 - 2 * core
     pos, grp = z % 4, z // 4
+    here = r * ND + d
     up, down = (z + 1) % NC, (z + NC - 1) % NC
     above, below, across = (r + 2) % NR, (r + NR - 2) % NR, (r + 4) % NR
     right, left = (d + 1) % ND, (d + ND - 1) % ND
@@ -62,6 +63,14 @@
     def go(copy):
         copy.start()
         started.append(copy)
+
+    def drain(left=0):
+        while len(started) > left:
+            started.pop(0).wait_send()
+
+    def tell(token, distance):
+        for peer in ((z + distance) % NC, (z + NC - distance) % NC):
+            pl.semaphore_signal(token, inc=1, device_id={"col": peer}, device_id_type=MESH)
 
     def arrived(ref, recv):
         remote(ref, ref, csend.at[0], recv, row=partner).wait_recv()
@@ -74,9 +83,9 @@
     load_block.start()
 
     barrier = pltpu.get_barrier_semaphore()
-    peers = [{"col": (z + k) % NC} for k in (1, 15, 2, 14, 3, 13)]
+    peers = [{"col": up}, {"col": down}]
     peers += [{"depth": (d + k) % ND} for k in range(1, ND)]
-    peers += [{"row": (r + k) % NR} for k in range(1, NR)]
+    peers += [{"row": above}, {"row": below}, {"row": across}, {"row": partner}]
     for peer in peers:
         pl.semaphore_signal(barrier, inc=1, device_id=peer, device_id_type=MESH)
     acc[...] = jnp.zeros_like(acc)
@@ -154,7 +163,11 @@
         block_send(across, q3, row=partner)
         block_wait(across, q2)
         block_send(across, q2, row=partner)
-        for b in (partner, (partner + 2) % NR, (partner + 4) % NR, (partner + 6) % NR):
+        for q in range(ND):
+            block_wait((partner + 4) % NR, q)
+
+    def near_blocks():
+        for b in (partner, (partner + 2) % NR, (partner + 6) % NR):
             for q in range(ND):
                 block_wait(b, q)
 
@@ -163,12 +176,23 @@
         right_op = blk[source // 2, at(source % 2, width), :]
         acc[lo:hi] += product3(left_op, right_op, NN)
 
+    def middle_chunks(ready, lo, hi):
+        def one(i, _):
+            source = (z + i + NC - 4) % NC
+
+            @pl.when((source // 4 != across // 2) == ready)
+            def _():
+                chunk(source, 0, part)
+
+            return 0
+
+        lax.fori_loop(lo, hi, one, 0)
+
     def chunks(k, lo=0, hi=part):
-        def one(i, _):
-            chunk((z + NC + k - 2 * k * i) % NC, lo, hi)
-            return 0
-
-        lax.fori_loop(0, 2, one, 0)
+        terms = []
+        for source in ((z + k) % NC, (z + NC - k) % NC):
+            terms.append(product3(zg[source, lo:hi], blk[source // 2, at(source % 2, width), :], NN))
+        acc[lo:hi] += terms[0] + terms[1]
 
     ring(0, EARLY)
     for k in range(1, ND):
@@ -187,14 +211,14 @@
         block_send(r, q, row=partner)
 
     ring(1, EARLY)
+    tell(token_2, 2)
     ring(1, LATE)
     for k, peer in enumerate((above, below, across)):
         arrived(zall.at[peer], grecv_r.at[peer])
         go(remote(zall.at[peer], zall.at[peer], gsend.at[8 + k], grecv_r.at[peer], row=partner))
     ring(2, EARLY)
-    far = [(z + 5) % NC, (z + NC - 5) % NC]
-    for peer in far:
-        pl.semaphore_signal(token, inc=1, device_id={"col": peer}, device_id_type=MESH)
+    pl.semaphore_wait(token_2, 2)
+    tell(token_4, 4)
 
     for peer in (partner, (partner + 2) % NR, (partner + 4) % NR, (partner + 6) % NR):
         arrived(zall.at[peer], grecv_r.at[peer])
@@ -212,32 +236,37 @@
     old = lax.dot_general(ones, s_hi, NT, preferred_element_type=F32) + lax.dot_general(
         ones, s_lo, NT, preferred_element_type=F32
     )
-    sx[d, 2] = old[0, :LANES]
-    sx[d, 3] = old[0, LANES:]
-    for k in range(1, 4):
-        q = (pos + k) % 4
-        go(remote(pst.at[d, q], r1.at[pos], psend.at[k - 1], precv1.at[pos], col=grp * 4 + q))
+    sx[here, 2] = old[0, :LANES]
+    sx[here, 3] = old[0, LANES:]
+    two_up, two_down = (z + 2) % NC, (z + NC - 2) % NC
+    low, high = pl.ds(0, 2), pl.ds(2, 2)
+    go(remote(pst.at[d, up % 4], r1.at[0], psend.at[0], precv1.at[0], col=up))
+    go(remote(pst.at[d, down % 4], r1.at[1], psend.at[1], precv1.at[1], col=down))
+    go(remote(pst.at[d, two_down % 4, low], r1.at[2, low], psend.at[2], precv1.at[2], col=two_down))
+    go(remote(pst.at[d, two_up % 4, high], r1.at[2, high], psend.at[6], precv1.at[3], col=two_up))
 
     ring(2, LATE)
     block_event_1()
     ring(3, EARLY)
     ring(3, LATE)
     block_event_2()
-    total = pst[d, pos]
-    for k in range(1, 4):
-        q = (pos + k) % 4
-        arrived(r1.at[q], precv1.at[q])
-        total = total + r1[q]
-    s1[...] = total
-    pl.semaphore_wait(token, 2)
+    arrived(r1.at[0], precv1.at[0])
+    arrived(r1.at[1], precv1.at[1])
+    arrived(r1.at[2, low], precv1.at[2])
+    arrived(r1.at[2, high], precv1.at[3])
+    s1[...] = (pst[d, pos] + r1[0]) + (r1[1] + r1[2])
+    pl.semaphore_wait(token_4, 2)
     for k in range(1, 4):
         q = (grp + k) % 4
         go(remote(s1.at[q], r2.at[grp], psend.at[2 + k], precv2.at[grp], col=q * 4 + pos))
     ring(4, EARLY)
-    ring(5, EARLY)
+    drain(60)
     ring(4, LATE)
     block_event_3()
-    ring(6, EARLY)
+    ring(5, EARLY)
+    near_blocks()
+    middle_chunks(True, 3, 6)
+    ring(5, LATE)
     new = s1[grp]
     for k in range(1, 4):
         q = (grp + k) % 4
@@ -246,37 +275,35 @@
     app[:, :LANES] = new[:own]
     app[:, LANES:] = new[own:]
     squares = new * new
-    sx[d, 0] = jnp.sum(squares[:own], axis=0)
-    sx[d, 1] = jnp.sum(squares[own:], axis=0)
-    for k in range(1, ND):
-        go(remote(sx.at[d], sx.at[d], ssend.at[k], srecv_x.at[d], depth=(d + k) % ND))
+    sx[here, 0] = jnp.sum(squares[:own], axis=0)
+    sx[here, 1] = jnp.sum(squares[own:], axis=0)
+    for k in range(1, NR * ND):
+        peer = (here + k) % (NR * ND)
+        go(remote(sx.at[here], sx.at[here], ssend.at[k], srecv_x.at[here], row=peer // ND, depth=peer % ND))
+    middle_chunks(True, 1, 3)
+    middle_chunks(True, 6, 8)
+    ring(6, EARLY)
     block_event_4()
-    chunk(z, 0, part)
-    chunks(1)
-    ring(5, LATE)
-    for k in range(1, ND):
-        q = (d + k) % ND
-        arrived(sx.at[q], srecv_x.at[q])
-    sr[r] = jnp.sum(sx[...], axis=0)
-    for k in range(1, NR):
-        go(remote(sr.at[r], sr.at[r], ssend.at[3 + k], srecv_r.at[r], row=(r + k) % NR))
-    chunks(2)
-    chunks(3)
-    ring(7, EARLY)
-    for k in range(1, NR):
-        q = (r + k) % NR
-        arrived(sr.at[q], srecv_r.at[q])
-    sums = jnp.sum(sr[...], axis=0)
+    middle_chunks(True, 0, 1)
+    middle_chunks(True, 8, 9)
+    middle_chunks(False, 0, 4)
+    ring(6, LATE)
+    for k in range(1, NR * ND):
+        peer = (here + k) % (NR * ND)
+        arrived(sx.at[peer], srecv_x.at[peer])
+    sums = jnp.sum(sx[...], axis=0)
     plane[0] = sums[0:2]
     plane[1] = sums[2:4]
     sz[z] = plane[core]
     for k in range(1, NC):
-        go(remote(sz.at[z], sz.at[z], ssend.at[10 + k], srecv_z.at[z], col=(z + k) % NC))
-    chunks(4)
+        go(remote(sz.at[z], sz.at[z], ssend.at[NR * ND + k], srecv_z.at[z], col=(z + k) % NC))
+    middle_chunks(False, 4, 9)
+    drain(60)
+    ring(7, EARLY)
     chunks(5)
-    ring(6, LATE)
+    ring(7, LATE)
     chunks(6)
-    chunks(7, 0, first)
+    chunks(7)
     ring(8, EARLY)
     chunk((z + 8) % NC, 0, first)
 
@@ -288,8 +315,6 @@
         q = (d + k) % ND
         go(remote(stage_e.at[q], cout_e.at[d], csend.at[k], crecv_e.at[d], depth=q))
     cout_e[d] = stage_e[d]
-    ring(7, LATE)
-    chunks(7, first, part)
     ring(8, LATE)
     chunk((z + 8) % NC, first, part)
     turned = acc[first:part].T
@@ -305,9 +330,8 @@
         q = (z + k) % NC
         arrived(sz.at[q], srecv_z.at[q])
     both[core] = jnp.sum(sz[...], axis=0)
-    go(remote(both.at[core], both.at[core], ssend.at[26], srecv_c, row=partner))
-    for copy in started:
-        copy.wait_send()
+    go(remote(both.at[core], both.at[core], ssend.at[0], srecv_c, row=partner))
+    drain()
     arrived(both.at[1 - core], srecv_c)
     nrm[...] = jnp.sqrt(both[0]) / jnp.sqrt(both[1] * (1.0 / (NR * ND)) + 1e-06)
     for k in range(1, ND):
@@ -352,11 +376,10 @@
             vmem(NR, rows, width),
             vmem(NR, ND, factor_cols, factor_rows),
             vmem(ND, 4, 4, 2 * own, LANES),
-            vmem(4, 4, 2 * own, LANES),
+            vmem(3, 4, 2 * own, LANES),
             vmem(4, 2 * own, LANES),
             vmem(4, 2 * own, LANES),
-            vmem(ND, 4, LANES),
-            vmem(NR, 4, LANES),
+            vmem(NR * ND, 4, LANES),
             vmem(2, 2, LANES),
             vmem(NC, 2, LANES),
             vmem(2, 2, LANES),
@@ -374,14 +397,14 @@
             dma((8,)),
             dma((4,)),
             dma((4,)),
-            dma((28,)),
-            dma((ND,)),
-            dma((NR,)),
+            dma((NR * ND + NC,)),
+            dma((NR * ND,)),
             dma((NC,)),
             dma,
             dma((8,)),
             dma((ND,)),
             dma((ND,)),
+            pltpu.SemaphoreType.REGULAR,
             pltpu.SemaphoreType.REGULAR,
         ],
         compiler_params=pltpu.CompilerParams(

time: 83.6 us -> 77.9 us (0.932)
  Pallas kernels: 81.7 us -> 76.3 us
    pallas_call x1, Pallas kernels: 80.9 us -> 75.5 us  [body(): pl.pallas_call(kernel, out_shape=(shape(ND, wide, LANES), shape(ND, wide...]
where the time goes in v3:
time: 77.9 us; the launch traced here: 77.7 us
  Pallas kernels  76.3 us (98%)
    pallas_call x1, Pallas kernels, body(): pl.pallas_call(kernel, out_shape=(shape(ND, wide, LANES), shape(ND, wide...  75.5 us

profile of v3, /device:TPU:1, one launch (start us, length us, event | category | flops | bytes accessed | tf_op | source)
XLA Modules:
  0.0 77.7 jit_solution(14283128958120390810)
XLA Ops:
  0.6 0.0 copy-start
  0.6 0.7 copy-done
  1.3 75.5 %shard_map.49 = (f32[4,96,128]{2,1,0:T(8,128)S(1)}, f32[4,48,128]{2,1,0:T(8,128)S(1)}, f32[12,256]{1,0:T(8,128)S(1)}, f32[2,128]{1,0:T(2,128)S(1)}) custom-call(f32[768,384]{1,0:T(8,128)} %a_hbm.1, f32[32,96]{1,0:T(8,128)S(1)} %bitcast.3), custom_call_target="tpu_custom_call" | custom-call | tf_op jit(solution)/shard_map/pallas_call | solution.py:369
  76.8 0.9 %shard_map.50 = (f32[96,768]{1,0:T(8,128)}, f32[12,256]{1,0:T(8,128)}, f32[2,128]{1,0:T(2,128)}) custom-call(f32[4,96,128]{2,1,0:T(8,128)S(1)} %get-tuple-element.10.early, f32[4,48,128]{2,1,0:T(8,128)S(1)} %get-tuple-element.11.late, f32[12,256]{1,0:T(8,128)S(1)} %get-tuple-element.12.app_in, f32[2,128]{1,0:T(2,128)S(1)} %get-tuple-element.13.nrm_in), custom_call_target="tpu_custom_call" | custom-call | tf_op jit(solution)/shard_map/pallas_call | solution.py:414
Async XLA Ops:
  0.6 0.7 copy-start

commit v4 on v3

--- a/solution.py
+++ b/solution.py
@@ -264,9 +264,6 @@
     ring(4, LATE)
     block_event_3()
     ring(5, EARLY)
-    near_blocks()
-    middle_chunks(True, 3, 6)
-    ring(5, LATE)
     new = s1[grp]
     for k in range(1, 4):
         q = (grp + k) % 4
@@ -280,14 +277,13 @@
     for k in range(1, NR * ND):
         peer = (here + k) % (NR * ND)
         go(remote(sx.at[here], sx.at[here], ssend.at[k], srecv_x.at[here], row=peer // ND, depth=peer % ND))
+    near_blocks()
+    middle_chunks(True, 3, 6)
+    ring(5, LATE)
     middle_chunks(True, 1, 3)
     middle_chunks(True, 6, 8)
     ring(6, EARLY)
     block_event_4()
-    middle_chunks(True, 0, 1)
-    middle_chunks(True, 8, 9)
-    middle_chunks(False, 0, 4)
-    ring(6, LATE)
     for k in range(1, NR * ND):
         peer = (here + k) % (NR * ND)
         arrived(sx.at[peer], srecv_x.at[peer])
@@ -297,6 +293,10 @@
     sz[z] = plane[core]
     for k in range(1, NC):
         go(remote(sz.at[z], sz.at[z], ssend.at[NR * ND + k], srecv_z.at[z], col=(z + k) % NC))
+    middle_chunks(True, 0, 1)
+    middle_chunks(True, 8, 9)
+    middle_chunks(False, 0, 4)
+    ring(6, LATE)
     middle_chunks(False, 4, 9)
     drain(60)
     ring(7, EARLY)

time: 77.9 us -> 77.6 us (level)
  no operation moved by 1% of the time
where the time goes in v4:
time: 77.6 us; the launch traced here: 77.4 us
  Pallas kernels  76 us (98%)
    pallas_call x1, Pallas kernels, body(): pl.pallas_call(kernel, out_shape=(shape(ND, wide, LANES), shape(ND, wide...  75.1 us

profile of v4, /device:TPU:1, one launch (start us, length us, event | category | flops | bytes accessed | tf_op | source)
XLA Modules:
  0.0 77.4 jit_solution(488128143793997633)
XLA Ops:
  0.6 0.0 copy-start
  0.6 0.7 copy-done
  1.3 75.1 %shard_map.49 = (f32[4,96,128]{2,1,0:T(8,128)S(1)}, f32[4,48,128]{2,1,0:T(8,128)S(1)}, f32[12,256]{1,0:T(8,128)S(1)}, f32[2,128]{1,0:T(2,128)S(1)}) custom-call(f32[768,384]{1,0:T(8,128)} %a_hbm.1, f32[32,96]{1,0:T(8,128)S(1)} %bitcast.3), custom_call_target="tpu_custom_call" | custom-call | tf_op jit(solution)/shard_map/pallas_call | solution.py:369
  76.5 0.9 %shard_map.50 = (f32[96,768]{1,0:T(8,128)}, f32[12,256]{1,0:T(8,128)}, f32[2,128]{1,0:T(2,128)}) custom-call(f32[4,96,128]{2,1,0:T(8,128)S(1)} %get-tuple-element.10.early, f32[4,48,128]{2,1,0:T(8,128)S(1)} %get-tuple-element.11.late, f32[12,256]{1,0:T(8,128)S(1)} %get-tuple-element.12.app_in, f32[2,128]{1,0:T(2,128)S(1)} %get-tuple-element.13.nrm_in), custom_call_target="tpu_custom_call" | custom-call | tf_op jit(solution)/shard_map/pallas_call | solution.py:414
Async XLA Ops:
  0.6 0.7 copy-start
